TPU v7x, 32 devices: a whole 2x2x4 slice. The times are simulated.
32 devices in a mesh: gx: 4 (over y, core), gy: 4 (over z), gz: 2 (over x).
Axes of the slice: x: 2, y: 2, z: 4, core: 2. Of those that a mesh axis runs over, the one named last changes fastest.
Arguments:
- residual: float32 [32, 128, 256], P('gx', 'gy', 'gz'), may hold values from -32 to 32
- direction: float32 [32, 128, 256], P('gx', 'gy', 'gz'), may hold values from -32 to 32
- diagonal: float32 [32, 128, 256], P('gx', 'gy', 'gz'), may hold values from 0.5 to 2
- recycled: bfloat16 [16, 32, 128, 256], P(None, 'gx', 'gy', 'gz'), may hold values from -6 to 6
- recycled_images: bfloat16 [16, 32, 128, 256], P(None, 'gx', 'gy', 'gz'), may hold values from -0.0014648438 to 0.0014648438
- coupling_inverse: float32 [16, 16], replicated, may hold values from -1 to 3, as said below
Outputs:
- solution_delta: float32 [32, 128, 256], P('gx', 'gy', 'gz')
- new_residual: float32 [32, 128, 256], P('gx', 'gy', 'gz')
- new_direction: float32 [32, 128, 256], P('gx', 'gy', 'gz')
Inputs may be any that keep to these rules, and one draw needn't show every extreme that they name: `coupling_inverse`: symmetric.
All inputs are finite; a program needn't handle non-finite values.
Results may differ from a plain program's by a relative error of at most 0.0028.
Values sent between devices are 32-bit elements; how exact they have to be, the bound alone decides.
No kernel may reach another device: no remote copies, remote signals or barrier semaphores. Data moves between devices by JAX's collectives and lax.ppermute only.
A program may use at most 64 MiB of HBM per device.

v0:
```python
import jax
import jax.numpy as jnp
import numpy as np
from jax import lax
from jax.sharding import PartitionSpec as P

S = 4
BASIS = 9
center = 7.25
half_width = 6.75


def extended(block, sides, width):
    for axis, dim in sides:
        count = lax.axis_size(axis)
        forward = [(i, i + 1) for i in range(count - 1)]
        forward.append((count - 1, 0))
        backward = [(target, source) for source, target in forward]
        low = lax.ppermute(
            lax.slice_in_dim(block, block.shape[dim] - width, None, axis=dim), axis, forward
        )
        high = lax.ppermute(lax.slice_in_dim(block, 0, width, axis=dim), axis, backward)
        block = jnp.concatenate([low, block, high], axis=dim)
    return block


def inside(padded):
    centre_cells = padded[:, 1:-1, 1:-1, 1:-1]
    beside_all = padded[:, 2:, 1:-1, 1:-1] + padded[:, :-2, 1:-1, 1:-1]
    beside_all = beside_all + padded[:, 1:-1, 2:, 1:-1] + padded[:, 1:-1, :-2, 1:-1]
    beside_all = beside_all + padded[:, 1:-1, 1:-1, 2:] + padded[:, 1:-1, 1:-1, :-2]
    return (centre_cells, beside_all)


def trim_margin(values, margin):
    if margin == 0:
        return values
    return values[..., margin:-margin, margin:-margin, margin:-margin]


def chebyshev_next(current, beside_all, diagonal, earlier):
    mapped = (6.0 + diagonal) * current - beside_all
    scaled = (mapped - center * current) / half_width
    if earlier is None:
        return scaled
    return 2.0 * scaled - earlier


def recurrence_matrix():
    recurrence = np.zeros((BASIS, BASIS), np.float32)
    for offset, length in ((0, S + 1), (S + 1, S)):
        recurrence[offset, offset] = center
        recurrence[offset + 1, offset] = half_width
        for column in range(1, length - 1):
            recurrence[offset + column + 1, offset + column] = half_width / 2
            recurrence[offset + column, offset + column] = center
            recurrence[offset + column - 1, offset + column] = half_width / 2
    return jnp.asarray(recurrence, dtype=jnp.float32)


def coordinates(totals, coupling_inverse):
    precise = lax.Precision.HIGHEST
    gram_block = totals[:BASIS]
    projections = totals[BASIS:]
    recurrence = recurrence_matrix()
    counter = jnp.arange(BASIS)
    residue = (counter == S + 1).astype(jnp.float32)
    search = (counter == 0).astype(jnp.float32)
    update = jnp.zeros((BASIS,), jnp.float32)
    norm_now = jnp.dot(residue, jnp.dot(gram_block, residue, precision=precise), precision=precise)
    for iteration in range(S):
        mapped = jnp.dot(recurrence, search, precision=precise)
        step_size = norm_now / jnp.dot(
            search, jnp.dot(gram_block, mapped, precision=precise), precision=precise
        )
        update = update + step_size * search
        residue = residue - step_size * mapped
        norm_next = jnp.dot(
            residue, jnp.dot(gram_block, residue, precision=precise), precision=precise
        )
        search = residue + norm_next / norm_now * search
        norm_now = norm_next
    weights = jnp.dot(
        coupling_inverse, jnp.dot(projections, residue, precision=precise), precision=precise
    )
    return (update, residue, search, weights.astype(jnp.bfloat16))


def body(residual, direction, diagonal, recycled, recycled_images, coupling_inverse):
    precise = lax.Precision.HIGHEST
    search_basis = [direction]
    residue_basis = [residual]
    earlier = None
    packed = jnp.stack([direction, residual, diagonal])
    padded = extended(packed, (("gx", 1), ("gy", 2), ("gz", 3)), S)
    wide_diag = padded[2]
    current = padded[:2]
    for iteration in range(S):
        if iteration == S - 1:
            current = current[:1]
            earlier = earlier[:1]
        centre_cells, beside_all = inside(current)
        margin = S - iteration - 1
        local_diag = trim_margin(wide_diag, iteration + 1)
        previous = None if earlier is None else trim_margin(earlier, 2)
        following = chebyshev_next(centre_cells, beside_all, local_diag, previous)
        earlier, current = (current, following)
        search_basis.append(trim_margin(following[0], margin))
        if following.shape[0] > 1:
            residue_basis.append(trim_margin(following[1], margin))
    basis = jnp.stack(search_basis + residue_basis)
    basis_flat = basis.reshape(basis.shape[0], -1)
    gram_block = lax.dot_general(
        basis_flat,
        basis_flat,
        (((1,), (1,)), ((), ())),
        precision=precise,
        preferred_element_type=jnp.float32,
    )
    rounded = basis_flat.astype(jnp.bfloat16)
    images = recycled_images.reshape(recycled_images.shape[0], -1)
    projections = lax.dot_general(
        images, rounded, (((1,), (1,)), ((), ())), preferred_element_type=jnp.float32
    )
    totals = lax.psum(jnp.concatenate([gram_block, projections], 0), ("gx", "gy", "gz"))
    update, residue, search, weights = coordinates(totals, coupling_inverse)
    shape = residual.shape
    solution_delta = jnp.dot(update, basis_flat, precision=precise).reshape(shape)
    new_residual = jnp.dot(residue, basis_flat, precision=precise).reshape(shape)
    correction = jnp.dot(
        weights, recycled.reshape(recycled.shape[0], -1), preferred_element_type=jnp.float32
    )
    new_direction = (jnp.dot(search, basis_flat, precision=precise) - correction).reshape(shape)
    return (solution_delta, new_residual, new_direction)


def solution(mesh):
    in_specs = (
        P("gx", "gy", "gz"),
        P("gx", "gy", "gz"),
        P("gx", "gy", "gz"),
        P(None, "gx", "gy", "gz"),
        P(None, "gx", "gy", "gz"),
        P(),
    )
    out_specs = (P("gx", "gy", "gz"), P("gx", "gy", "gz"), P("gx", "gy", "gz"))
    return jax.shard_map(body, mesh=mesh, in_specs=in_specs, out_specs=out_specs, check_vma=False)
```

profile of v0, /device:TPU:0, one launch (start us, length us, event | category | flops | bytes accessed | tf_op | source)
XLA Modules:
  0.0 110.9 jit_solution(13209403578807758797)
XLA Ops:
  0.7 1.1 %pad_maximum_fusion.2 = f32[3,8,32,128]{3,2,1,0:T(8,128)S(1)} fusion(f32[1,8,32,128]{3,2,1,0:T(8,128)} %bitcast.257, f32[1,8,32,128]{3,2,1,0:T(8,128)} %bitcast.251, f32[1,8,32,128]{3,2,1,0:T(8,128)} %bitcast.245), kind=kLoop, calls=%fused_computation.81 | loop fusion | flops 196608 | bytes 786432 | tf_op jit(solution)/shard_map/stack | solution.py:94
  2.4 2.0 %collective-permute-start.1 = (f32[3,4,32,128]{3,2,1,0:T(8,128)S(1)}, f32[3,4,32,128]{3,2,1,0:T(8,128)S(1)}, u32[]{:S(2)}, u32[]{:S(2)}) collective-permute-start(f32[3,4,32,128]{3,2,1,0:T(8,128)S(1)} %get-tuple-element.14), channel_id=1, source_target_pairs={{8,0},{16,8},{24,16},{0,24},{9,1},{17,9},{25,17},{1,25},{10,2},{18... | collective-permute-start | bytes 589832 | tf_op jit(solution)/shard_map/ppermute | solution.py:22
  4.4 3.3 %collective-permute-done = f32[3,4,32,128]{3,2,1,0:T(8,128)S(1)} collective-permute-done((f32[3,4,32,128]{3,2,1,0:T(8,128)S(1)}, f32[3,4,32,128]{3,2,1,0:T(8,128)S(1)}, u32[]{:S(2)}, u32[]{:S(2)}) %collective-permute-start) | collective-permute-done | bytes 196640 | tf_op jit(solution)/shard_map/ppermute | solution.py:19
  7.7 1.9 %collective-permute-done.1 = f32[3,4,32,128]{3,2,1,0:T(8,128)S(1)} collective-permute-done((f32[3,4,32,128]{3,2,1,0:T(8,128)S(1)}, f32[3,4,32,128]{3,2,1,0:T(8,128)S(1)}, u32[]{:S(2)}, u32[]{:S(2)}) %collective-permute-start.1) | collective-permute-done | bytes 196640 | tf_op jit(solution)/shard_map/ppermute | solution.py:22
  9.6 0.9 pad_maximum_fusion.7
  10.5 1.6 %collective-permute-start.2 = (f32[3,16,4,128]{3,2,1,0:T(4,128)S(1)}, f32[3,16,4,128]{3,2,1,0:T(4,128)S(1)}, u32[]{:S(2)}, u32[]{:S(2)}) collective-permute-start(f32[3,16,4,128]{3,2,1,0:T(4,128)S(1)} %get-tuple-element.11), channel_id=1, source_target_pairs={{0,2},{2,4},{4,6},{6,0},{1,3},{3,5},{5,7},{7,1},{8,10},{10,12},{12... | collective-permute-start | bytes 294920 | tf_op jit(solution)/shard_map/ppermute | solution.py:19
  12.1 2.2 %collective-permute-start.3 = (f32[3,16,4,128]{3,2,1,0:T(4,128)S(1)}, f32[3,16,4,128]{3,2,1,0:T(4,128)S(1)}, u32[]{:S(2)}, u32[]{:S(2)}) collective-permute-start(f32[3,16,4,128]{3,2,1,0:T(4,128)S(1)} %get-tuple-element.12), channel_id=1, source_target_pairs={{2,0},{4,2},{6,4},{0,6},{3,1},{5,3},{7,5},{1,7},{10,8},{12,10},{14... | collective-permute-start | bytes 294920 | tf_op jit(solution)/shard_map/ppermute | solution.py:22
  14.4 3.7 %collective-permute-done.2 = f32[3,16,4,128]{3,2,1,0:T(4,128)S(1)} collective-permute-done((f32[3,16,4,128]{3,2,1,0:T(4,128)S(1)}, f32[3,16,4,128]{3,2,1,0:T(4,128)S(1)}, u32[]{:S(2)}, u32[]{:S(2)}) %collective-permute-start.2) | collective-permute-done | bytes 98336 | tf_op jit(solution)/shard_map/ppermute | solution.py:19
  18.0 1.4 %collective-permute-done.3 = f32[3,16,4,128]{3,2,1,0:T(4,128)S(1)} collective-permute-done((f32[3,16,4,128]{3,2,1,0:T(4,128)S(1)}, f32[3,16,4,128]{3,2,1,0:T(4,128)S(1)}, u32[]{:S(2)}, u32[]{:S(2)}) %collective-permute-start.3) | collective-permute-done | bytes 98336 | tf_op jit(solution)/shard_map/ppermute | solution.py:22
  20.3 1.6 %collective-permute-start.4 = (f32[3,16,40,4]{2,1,3,0:T(8,128)S(1)}, f32[3,16,40,4]{2,1,3,0:T(8,128)S(1)}, u32[]{:S(2)}, u32[]{:S(2)}) collective-permute-start(f32[3,16,40,4]{2,1,3,0:T(8,128)S(1)} %copy.18), channel_id=1, source_target_pairs={{0,1},{1,0},{2,3},{3,2},{4,5},{5,4},{6,7},{7,6},{8,9},{9,8},{10,11... | collective-permute-start | bytes 92168 | tf_op jit(solution)/shard_map/ppermute | solution.py:19
  22.9 2.8 %collective-permute-done.4 = f32[3,16,40,4]{2,1,3,0:T(8,128)S(1)} collective-permute-done((f32[3,16,40,4]{2,1,3,0:T(8,128)S(1)}, f32[3,16,40,4]{2,1,3,0:T(8,128)S(1)}, u32[]{:S(2)}, u32[]{:S(2)}) %collective-permute-start.4) | collective-permute-done | bytes 30752 | tf_op jit(solution)/shard_map/ppermute | solution.py:19
  26.1 1.0 collective-permute-done.5
  27.5 1.1 pad_maximum_fusion
  29.2 1.9 %fusion.6 = f32[2,14,38,134]{3,2,1,0:T(8,128)S(1)} fusion(f32[3,16,40,136]{3,2,1,0:T(8,128)S(1)} %pad_maximum_fusion, f32[14,38,134]{2,1,0:T(8,128)S(1)} %slice_add_fusion.15), kind=kLoop, calls=%fused_computation.8 | loop fusion | flops 1425760 | bytes 4847584 | tf_op jit(solution)/shard_map/div | solution.py:43
  31.1 1.9 %slice_subtract_fusion = f32[2,12,36,132]{3,2,1,0:T(8,128)S(1)} fusion(f32[3,16,40,136]{3,2,1,0:T(8,128)S(1)} %pad_maximum_fusion, f32[2,14,38,134]{3,2,1,0:T(8,128)S(1)} %fusion.6, f32[12,36,132]{2,1,0:T(8,128)S(1)} %slice_add_fusion.16), kind=kLoop, calls=%fused_computation.43 | loop fusion | flops 1254528 | bytes 4333824 | tf_op jit(solution)/shard_map/sub | solution.py:46
  33.0 1.6 %slice_subtract_fusion.1 = f32[2,10,34,130]{3,2,1,0:T(8,128)S(1)} fusion(f32[2,14,38,134]{3,2,1,0:T(8,128)S(1)} %fusion.6, f32[2,12,36,132]{3,2,1,0:T(8,128)S(1)} %slice_subtract_fusion, f32[10,34,130]{2,1,0:T(8,128)S(1)} %slice_add_fusion.17), kind=kLoop, calls=%fused_computation.53 | loop fusion | flops 972400 | bytes 3359200 | tf_op jit(solution)/shard_map/sub | solution.py:46
  35.8 2.1 %stack.65 = f32[9,8,32,128]{3,0,2,1:T(8,128)S(1)} concatenate(f32[1,8,32,128]{3,0,2,1:T(1,128)S(1)} %bitcast.249, f32[1,8,32,128]{3,0,2,1:T(1,128)S(1)} %bitcast.273, f32[1,8,32,128]{3,0,2,1:T(1,128)S(1)} %bitcast.267, f32[1,8,32,128]{3,0,2,1:T(1,128)S(1)} %bitcast.263, f32[1,8,32,128]{3,0,2,1:T(1,128)S(1)} %bitcast.261, f32[1,8,32,128]{3,0,2,1:T(1,128)S(1)} %bitcast.255, ...), dimensions={0} | concatenate | bytes 2359296 | tf_op jit(solution)/shard_map/stack | solution.py:111
  37.8 2.9 %convolution_bitcast_fusion.1 = f32[9,9]{0,1:T(8,128)S(1)} fusion(f32[9,8,32,128]{3,0,2,1:T(8,128)S(1)} %stack.65), kind=kOutput, calls=%fused_computation.14 | convolution fusion | flops 31850496 | bytes 1179972 | tf_op jit(solution)/shard_map/dot_general | solution.py:113
  40.7 1.9 %stack.75 = f32[9,32768]{1,0:T(8,128)S(1)} concatenate(f32[1,32768]{1,0:T(1,128)S(1)} %bitcast.250, f32[1,32768]{1,0:T(1,128)S(1)} %bitcast.274, f32[1,32768]{1,0:T(1,128)S(1)} %bitcast.268, f32[1,32768]{1,0:T(1,128)S(1)} %bitcast.264, f32[1,32768]{1,0:T(1,128)S(1)} %bitcast.262, f32[1,32768]{1,0:T(1,128)S(1)} %bitcast.256, f32[1,32768]{1,0:T(1,128)S(1)} %bitcast.272, ...), dimensions={0} | concatenate | bytes 2359296 | tf_op jit(solution)/shard_map/stack | solution.py:111
  42.6 2.0 %convolution_bitcast_fusion = f32[16,9]{0,1:T(8,128)S(1)} fusion(bf16[2,8,256,128]{3,2,1,0:T(8,128)(2,1)} %bitcast.275, f32[9,32768]{1,0:T(8,128)S(1)} %stack.75), kind=kOutput, calls=%fused_computation.13 | convolution fusion | flops 9732096 | bytes 2228800 | tf_op jit(solution)/shard_map/dot_general | solution.py:122
  44.7 40.0 %psum.7 = f32[25,9]{0,1:T(8,128)S(1)} all-reduce(f32[25,9]{0,1:T(8,128)S(1)} %pad_maximum_fusion.8), channel_id=1, replica_groups=mesh['gx'=4,'gy'=4,'gz'=2] {'gx','gy','gz'}, use_global_device_ids=true, to_apply=%region_0.0 | all-reduce | flops 225 | bytes 1800 | tf_op jit(solution)/shard_map/psum | solution.py:125
  102.1 2.4 %fusion = f32[1,8,32,128]{3,0,2,1:T(1,128)} fusion(f32[8,32,128,9]{2,1,0,3:T(8,128)S(1)} %bitcast.242, f32[9]{0:T(128)S(1)} %fusion.67), kind=kOutput, calls=%fused_computation | convolution fusion | flops 3538944 | bytes 1310756 | tf_op jit(solution)/shard_map/dot_general | solution.py:129
  104.5 2.4 %fusion.2 = f32[1,8,32,128]{3,0,2,1:T(1,128)} fusion(f32[8,32,128,9]{2,1,0,3:T(8,128)S(1)} %bitcast.243, f32[9]{0:T(128)S(1)} %multiply_add_fusion, f32[9]{0:T(128)S(1)} %multiply_add_fusion.1, f32[9]{0:T(128)S(1)} %select_add_fusion, f32[]{:T(128)S(6)} %div.44, f32[]{:T(128)S(6)} %div.42, f32[]{:T(128)S(6)} %div.40, f32[]{:T(128)S(6)} %div.38), kind=kOutput, calls=%fused_computation.2 | convolution fusion | flops 3539016 | bytes 1310844 | tf_op jit(solution)/shard_map/dot_general | solution.py:128
  108.3 1.1 %fusion.62 = f32[1,32768]{1,0:T(1,128)S(1)} fusion(f32[9,32768]{1,0:T(8,128)S(1)} %stack.75, f32[9]{0:T(128)S(1)} %fusion.67, f32[9]{0:T(128)S(1)} %multiply_add_fusion, f32[]{:T(128)S(6)} %div.45), kind=kOutput, calls=%fused_computation.119 | convolution fusion | flops 3538962 | bytes 1310796 | tf_op jit(solution)/shard_map/dot_general | solution.py:133
  (61 shorter events, 14.6 us)
Async XLA Ops:
  0.6 108.8 %copy-start = (f32[16,16]{1,0:T(8,128)S(1)}, f32[16,16]{1,0:T(8,128)}, u32[]{:S(2)}) copy-start(f32[16,16]{1,0:T(8,128)} %param.12) | copy-start | bytes 3076
  0.6 18.8 %copy-start.1 = (f32[8,32,128]{2,1,0:T(8,128)S(1)}, f32[8,32,128]{2,1,0:T(8,128)}, u32[]{:S(2)}) copy-start(f32[8,32,128]{2,1,0:T(8,128)} %param.8) | copy-start | bytes 393220
  0.7 18.8 %copy-start.2 = (f32[8,32,128]{2,1,0:T(8,128)S(1)}, f32[8,32,128]{2,1,0:T(8,128)}, u32[]{:S(2)}) copy-start(f32[8,32,128]{2,1,0:T(8,128)} %param.7) | copy-start | bytes 393220
  0.7 18.8 %copy-start.3 = (f32[8,32,128]{2,1,0:T(8,128)S(1)}, f32[8,32,128]{2,1,0:T(8,128)}, u32[]{:S(2)}) copy-start(f32[8,32,128]{2,1,0:T(8,128)} %param.9) | copy-start | bytes 393220
  1.8 5.8 %collective-permute-start = (f32[3,4,32,128]{3,2,1,0:T(8,128)S(1)}, f32[3,4,32,128]{3,2,1,0:T(8,128)S(1)}, u32[]{:S(2)}, u32[]{:S(2)}) collective-permute-start(f32[3,4,32,128]{3,2,1,0:T(8,128)S(1)} %get-tuple-element.13), channel_id=1, source_target_pairs={{0,8},{8,16},{16,24},{24,0},{1,9},{9,17},{17,25},{25,1},{2,10},{10... | collective-permute-start | bytes 589832 | tf_op jit(solution)/shard_map/ppermute | solution.py:19
  2.4 7.2 %collective-permute-start.1 = (f32[3,4,32,128]{3,2,1,0:T(8,128)S(1)}, f32[3,4,32,128]{3,2,1,0:T(8,128)S(1)}, u32[]{:S(2)}, u32[]{:S(2)}) collective-permute-start(f32[3,4,32,128]{3,2,1,0:T(8,128)S(1)} %get-tuple-element.14), channel_id=1, source_target_pairs={{8,0},{16,8},{24,16},{0,24},{9,1},{17,9},{25,17},{1,25},{10,2},{18... | collective-permute-start | bytes 589832 | tf_op jit(solution)/shard_map/ppermute | solution.py:22
  10.5 7.5 %collective-permute-start.2 = (f32[3,16,4,128]{3,2,1,0:T(4,128)S(1)}, f32[3,16,4,128]{3,2,1,0:T(4,128)S(1)}, u32[]{:S(2)}, u32[]{:S(2)}) collective-permute-start(f32[3,16,4,128]{3,2,1,0:T(4,128)S(1)} %get-tuple-element.11), channel_id=1, source_target_pairs={{0,2},{2,4},{4,6},{6,0},{1,3},{3,5},{5,7},{7,1},{8,10},{10,12},{12... | collective-permute-start | bytes 294920 | tf_op jit(solution)/shard_map/ppermute | solution.py:19
  12.1 7.3 %collective-permute-start.3 = (f32[3,16,4,128]{3,2,1,0:T(4,128)S(1)}, f32[3,16,4,128]{3,2,1,0:T(4,128)S(1)}, u32[]{:S(2)}, u32[]{:S(2)}) collective-permute-start(f32[3,16,4,128]{3,2,1,0:T(4,128)S(1)} %get-tuple-element.12), channel_id=1, source_target_pairs={{2,0},{4,2},{6,4},{0,6},{3,1},{5,3},{7,5},{1,7},{10,8},{12,10},{14... | collective-permute-start | bytes 294920 | tf_op jit(solution)/shard_map/ppermute | solution.py:22
  19.9 2.9 %copy-start.5 = (f32[9,9]{1,0:T(8,128)S(1)}, f32[9,9]{1,0:T(8,128)}, u32[]{:S(2)}) copy-start(f32[9,9]{1,0:T(8,128)} %constant.17.clone) | copy-start | bytes 976
  20.3 5.4 %collective-permute-start.4 = (f32[3,16,40,4]{2,1,3,0:T(8,128)S(1)}, f32[3,16,40,4]{2,1,3,0:T(8,128)S(1)}, u32[]{:S(2)}, u32[]{:S(2)}) collective-permute-start(f32[3,16,40,4]{2,1,3,0:T(8,128)S(1)} %copy.18), channel_id=1, source_target_pairs={{0,1},{1,0},{2,3},{3,2},{4,5},{5,4},{6,7},{7,6},{8,9},{9,8},{10,11... | collective-permute-start | bytes 92168 | tf_op jit(solution)/shard_map/ppermute | solution.py:19
  22.2 4.9 %collective-permute-start.5 = (f32[3,16,40,4]{2,1,3,0:T(8,128)S(1)}, f32[3,16,40,4]{2,1,3,0:T(8,128)S(1)}, u32[]{:S(2)}, u32[]{:S(2)}) collective-permute-start(f32[3,16,40,4]{2,1,3,0:T(8,128)S(1)} %copy.19), channel_id=1, source_target_pairs={{1,0},{0,1},{3,2},{2,3},{5,4},{4,5},{7,6},{6,7},{9,8},{8,9},{11,10... | collective-permute-start | bytes 92168 | tf_op jit(solution)/shard_map/ppermute | solution.py:22
  104.5 5.1 %copy-start.4 = (bf16[16,8,32,128]{3,2,1,0:T(8,128)(2,1)S(1)}, bf16[16,8,32,128]{3,2,1,0:T(8,128)(2,1)}, u32[]{:S(2)}) copy-start(bf16[16,8,32,128]{3,2,1,0:T(8,128)(2,1)} %param.10) | copy-start | bytes 3145732
where the time goes:
time: 111 us
  blocking collectives  40 us (36%)
  matrix products  19.1 us (17%)
  waiting for transfers between devices  14 us (13%)
  between operations  11.8 us (11%)
  other arithmetic  10.2 us (9%)
  starting transfers between devices  8.58 us (8%)
  local copies, waits for them, and re-layouts  7.23 us (7%)
    psum x1, blocking collectives, body(): lax.psum(jnp.concatenate([gram_block, projections], 0), ('gx', 'gy', 'gz'))  40 us
    ppermute x3, waiting for transfers between devices, extended(): lax.ppermute(lax.slice_in_dim(block, block.shape[dim] - width, None, axis...  9.69 us
    ppermute x3, starting transfers between devices, extended(): lax.ppermute(lax.slice_in_dim(block, 0, width, axis=dim), axis, backward)  4.85 us
    ppermute x3, waiting for transfers between devices, extended(): lax.ppermute(lax.slice_in_dim(block, 0, width, axis=dim), axis, backward)  4.3 us
    another operation x2, local copies, waits for them, and re-layouts, body(): basis = jnp.stack(search_basis + residue_basis)  3.93 us
    sub x3, other arithmetic, chebyshev_next(): return 2.0 * scaled - earlier  3.83 us
    dot_general x5, matrix products, coordinates(): jnp.dot(gram_block, residue, precision=precise)  3.78 us
    ppermute x3, starting transfers between devices, extended(): lax.ppermute(lax.slice_in_dim(block, block.shape[dim] - width, None, axis...  3.73 us
  transfers between devices with their start and end apart: 6, of which 6 were waited for; matrix products, arithmetic and copies ran while one was open for 1% of the time, Pallas kernels for 0%

commit v1 on v0

--- a/solution.py
+++ b/solution.py
@@ -122,7 +122,12 @@
     projections = lax.dot_general(
         images, rounded, (((1,), (1,)), ((), ())), preferred_element_type=jnp.float32
     )
-    totals = lax.psum(jnp.concatenate([gram_block, projections], 0), ("gx", "gy", "gz"))
+
+    def proceed_stops_all(page):
+        prior = jnp.sum(lax.all_gather(page, ("gx", "gy", "gz")), axis=0)
+        return prior
+
+    totals = proceed_stops_all(jnp.concatenate([gram_block, projections], 0))
     update, residue, search, weights = coordinates(totals, coupling_inverse)
     shape = residual.shape
     solution_delta = jnp.dot(update, basis_flat, precision=precise).reshape(shape)

time: 111 us -> 138 us (1.24)
  blocking collectives: 40 us -> 66.7 us
    all_gather x0 -> x1, blocking collectives: none -> 66.7 us  [proceed_stops_all(): prior = jnp.sum(lax.all_gather(page, ('gx', 'gy', 'gz')), axis=0)]
    psum x1 -> x0, blocking collectives: 40 us -> none  [body(): lax.psum(jnp.concatenate([gram_block, projections], 0), ('gx', 'gy', 'gz'))]
where the time goes in v1:
time: 138 us
  blocking collectives  66.7 us (48%)
  matrix products  19.1 us (14%)
  waiting for transfers between devices  14 us (10%)
  between operations  11.8 us (9%)
  other arithmetic  10.3 us (7%)
  starting transfers between devices  8.58 us (6%)
  local copies, waits for them, and re-layouts  7.23 us (5%)
    all_gather x1, blocking collectives, proceed_stops_all(): prior = jnp.sum(lax.all_gather(page, ('gx', 'gy', 'gz')), axis=0)  66.7 us
    ppermute x3, waiting for transfers between devices, extended(): lax.ppermute(lax.slice_in_dim(block, block.shape[dim] - width, None, axis...  9.69 us
    ppermute x3, starting transfers between devices, extended(): lax.ppermute(lax.slice_in_dim(block, 0, width, axis=dim), axis, backward)  4.85 us
    ppermute x3, waiting for transfers between devices, extended(): lax.ppermute(lax.slice_in_dim(block, 0, width, axis=dim), axis, backward)  4.3 us
    another operation x2, local copies, waits for them, and re-layouts, body(): basis = jnp.stack(search_basis + residue_basis)  3.93 us
    sub x3, other arithmetic, chebyshev_next(): return 2.0 * scaled - earlier  3.83 us
    dot_general x5, matrix products, coordinates(): jnp.dot(gram_block, residue, precision=precise)  3.78 us
    ppermute x3, starting transfers between devices, extended(): lax.ppermute(lax.slice_in_dim(block, block.shape[dim] - width, None, axis...  3.73 us
  transfers between devices with their start and end apart: 6, of which 6 were waited for; matrix products, arithmetic and copies ran while one was open for 1% of the time, Pallas kernels for 0%

profile of v1, /device:TPU:0, one launch (start us, length us, event | category | flops | bytes accessed | tf_op | source)
XLA Modules:
  0.0 137.6 jit_solution(17090647900251413648)
XLA Ops:
  0.7 1.1 pad_maximum_fusion.2
  2.4 2.0 %collective-permute-start.1 = (f32[3,4,32,128]{3,2,1,0:T(8,128)S(1)}, f32[3,4,32,128]{3,2,1,0:T(8,128)S(1)}, u32[]{:S(2)}, u32[]{:S(2)}) collective-permute-start(f32[3,4,32,128]{3,2,1,0:T(8,128)S(1)} %get-tuple-element.14), channel_id=1, source_target_pairs={{8,0},{16,8},{24,16},{0,24},{9,1},{17,9},{25,17},{1,25},{10,2},{18... | collective-permute-start | bytes 589832 | tf_op jit(solution)/shard_map/ppermute | solution.py:22
  4.4 3.3 %collective-permute-done = f32[3,4,32,128]{3,2,1,0:T(8,128)S(1)} collective-permute-done((f32[3,4,32,128]{3,2,1,0:T(8,128)S(1)}, f32[3,4,32,128]{3,2,1,0:T(8,128)S(1)}, u32[]{:S(2)}, u32[]{:S(2)}) %collective-permute-start) | collective-permute-done | bytes 196640 | tf_op jit(solution)/shard_map/ppermute | solution.py:19
  7.7 1.9 %collective-permute-done.1 = f32[3,4,32,128]{3,2,1,0:T(8,128)S(1)} collective-permute-done((f32[3,4,32,128]{3,2,1,0:T(8,128)S(1)}, f32[3,4,32,128]{3,2,1,0:T(8,128)S(1)}, u32[]{:S(2)}, u32[]{:S(2)}) %collective-permute-start.1) | collective-permute-done | bytes 196640 | tf_op jit(solution)/shard_map/ppermute | solution.py:22
  9.6 0.9 pad_maximum_fusion.7
  10.5 1.6 %collective-permute-start.2 = (f32[3,16,4,128]{3,2,1,0:T(4,128)S(1)}, f32[3,16,4,128]{3,2,1,0:T(4,128)S(1)}, u32[]{:S(2)}, u32[]{:S(2)}) collective-permute-start(f32[3,16,4,128]{3,2,1,0:T(4,128)S(1)} %get-tuple-element.11), channel_id=1, source_target_pairs={{0,2},{2,4},{4,6},{6,0},{1,3},{3,5},{5,7},{7,1},{8,10},{10,12},{12... | collective-permute-start | bytes 294920 | tf_op jit(solution)/shard_map/ppermute | solution.py:19
  12.1 2.2 %collective-permute-start.3 = (f32[3,16,4,128]{3,2,1,0:T(4,128)S(1)}, f32[3,16,4,128]{3,2,1,0:T(4,128)S(1)}, u32[]{:S(2)}, u32[]{:S(2)}) collective-permute-start(f32[3,16,4,128]{3,2,1,0:T(4,128)S(1)} %get-tuple-element.12), channel_id=1, source_target_pairs={{2,0},{4,2},{6,4},{0,6},{3,1},{5,3},{7,5},{1,7},{10,8},{12,10},{14... | collective-permute-start | bytes 294920 | tf_op jit(solution)/shard_map/ppermute | solution.py:22
  14.4 3.7 %collective-permute-done.2 = f32[3,16,4,128]{3,2,1,0:T(4,128)S(1)} collective-permute-done((f32[3,16,4,128]{3,2,1,0:T(4,128)S(1)}, f32[3,16,4,128]{3,2,1,0:T(4,128)S(1)}, u32[]{:S(2)}, u32[]{:S(2)}) %collective-permute-start.2) | collective-permute-done | bytes 98336 | tf_op jit(solution)/shard_map/ppermute | solution.py:19
  18.0 1.4 %collective-permute-done.3 = f32[3,16,4,128]{3,2,1,0:T(4,128)S(1)} collective-permute-done((f32[3,16,4,128]{3,2,1,0:T(4,128)S(1)}, f32[3,16,4,128]{3,2,1,0:T(4,128)S(1)}, u32[]{:S(2)}, u32[]{:S(2)}) %collective-permute-start.3) | collective-permute-done | bytes 98336 | tf_op jit(solution)/shard_map/ppermute | solution.py:22
  20.3 1.6 %collective-permute-start.4 = (f32[3,16,40,4]{2,1,3,0:T(8,128)S(1)}, f32[3,16,40,4]{2,1,3,0:T(8,128)S(1)}, u32[]{:S(2)}, u32[]{:S(2)}) collective-permute-start(f32[3,16,40,4]{2,1,3,0:T(8,128)S(1)} %copy.18), channel_id=1, source_target_pairs={{0,1},{1,0},{2,3},{3,2},{4,5},{5,4},{6,7},{7,6},{8,9},{9,8},{10,11... | collective-permute-start | bytes 92168 | tf_op jit(solution)/shard_map/ppermute | solution.py:19
  22.9 2.8 %collective-permute-done.4 = f32[3,16,40,4]{2,1,3,0:T(8,128)S(1)} collective-permute-done((f32[3,16,40,4]{2,1,3,0:T(8,128)S(1)}, f32[3,16,40,4]{2,1,3,0:T(8,128)S(1)}, u32[]{:S(2)}, u32[]{:S(2)}) %collective-permute-start.4) | collective-permute-done | bytes 30752 | tf_op jit(solution)/shard_map/ppermute | solution.py:19
  26.1 1.0 collective-permute-done.5
  27.5 1.1 pad_maximum_fusion
  29.2 1.9 %fusion.6 = f32[2,14,38,134]{3,2,1,0:T(8,128)S(1)} fusion(f32[3,16,40,136]{3,2,1,0:T(8,128)S(1)} %pad_maximum_fusion, f32[14,38,134]{2,1,0:T(8,128)S(1)} %slice_add_fusion.15), kind=kLoop, calls=%fused_computation.8 | loop fusion | flops 1425760 | bytes 4847584 | tf_op jit(solution)/shard_map/div | solution.py:43
  31.1 1.9 %slice_subtract_fusion = f32[2,12,36,132]{3,2,1,0:T(8,128)S(1)} fusion(f32[3,16,40,136]{3,2,1,0:T(8,128)S(1)} %pad_maximum_fusion, f32[2,14,38,134]{3,2,1,0:T(8,128)S(1)} %fusion.6, f32[12,36,132]{2,1,0:T(8,128)S(1)} %slice_add_fusion.16), kind=kLoop, calls=%fused_computation.43 | loop fusion | flops 1254528 | bytes 4333824 | tf_op jit(solution)/shard_map/sub | solution.py:46
  33.0 1.6 %slice_subtract_fusion.1 = f32[2,10,34,130]{3,2,1,0:T(8,128)S(1)} fusion(f32[2,14,38,134]{3,2,1,0:T(8,128)S(1)} %fusion.6, f32[2,12,36,132]{3,2,1,0:T(8,128)S(1)} %slice_subtract_fusion, f32[10,34,130]{2,1,0:T(8,128)S(1)} %slice_add_fusion.17), kind=kLoop, calls=%fused_computation.53 | loop fusion | flops 972400 | bytes 3359200 | tf_op jit(solution)/shard_map/sub | solution.py:46
  35.8 2.1 %stack.65 = f32[9,8,32,128]{3,0,2,1:T(8,128)S(1)} concatenate(f32[1,8,32,128]{3,0,2,1:T(1,128)S(1)} %bitcast.251, f32[1,8,32,128]{3,0,2,1:T(1,128)S(1)} %bitcast.275, f32[1,8,32,128]{3,0,2,1:T(1,128)S(1)} %bitcast.269, f32[1,8,32,128]{3,0,2,1:T(1,128)S(1)} %bitcast.265, f32[1,8,32,128]{3,0,2,1:T(1,128)S(1)} %bitcast.263, f32[1,8,32,128]{3,0,2,1:T(1,128)S(1)} %bitcast.257, ...), dimensions={0} | concatenate | bytes 2359296 | tf_op jit(solution)/shard_map/stack | solution.py:111
  37.8 2.9 %convolution_bitcast_fusion.1 = f32[9,9]{0,1:T(8,128)S(1)} fusion(f32[9,8,32,128]{3,0,2,1:T(8,128)S(1)} %stack.65), kind=kOutput, calls=%fused_computation.14 | convolution fusion | flops 31850496 | bytes 1179972 | tf_op jit(solution)/shard_map/dot_general | solution.py:113
  40.7 1.9 %stack.75 = f32[9,32768]{1,0:T(8,128)S(1)} concatenate(f32[1,32768]{1,0:T(1,128)S(1)} %bitcast.252, f32[1,32768]{1,0:T(1,128)S(1)} %bitcast.276, f32[1,32768]{1,0:T(1,128)S(1)} %bitcast.270, f32[1,32768]{1,0:T(1,128)S(1)} %bitcast.266, f32[1,32768]{1,0:T(1,128)S(1)} %bitcast.264, f32[1,32768]{1,0:T(1,128)S(1)} %bitcast.258, f32[1,32768]{1,0:T(1,128)S(1)} %bitcast.274, ...), dimensions={0} | concatenate | bytes 2359296 | tf_op jit(solution)/shard_map/stack | solution.py:111
  42.6 2.0 %convolution_bitcast_fusion = f32[16,9]{0,1:T(8,128)S(1)} fusion(bf16[2,8,256,128]{3,2,1,0:T(8,128)(2,1)} %bitcast.277, f32[9,32768]{1,0:T(8,128)S(1)} %stack.75), kind=kOutput, calls=%fused_computation.13 | convolution fusion | flops 9732096 | bytes 2228800 | tf_op jit(solution)/shard_map/dot_general | solution.py:122
  44.7 66.7 %all-gather.1 = f32[32,25,9]{1,2,0:T(8,128)S(1)} all-gather(f32[1,25,9]{1,2,0:T(8,128)S(1)} %maximum_bitcast_fusion), channel_id=2, replica_groups=mesh['gx'=4,'gy'=4,'gz'=2] {'gx','gy','gz'}, dimensions={0}, use_global_device_ids=true | all-gather | bytes 29700 | tf_op jit(solution)/shard_map/all_gather | solution.py:127
  128.8 2.4 %fusion = f32[1,8,32,128]{3,0,2,1:T(1,128)} fusion(f32[8,32,128,9]{2,1,0,3:T(8,128)S(1)} %bitcast.244, f32[9]{0:T(128)S(1)} %fusion.67), kind=kOutput, calls=%fused_computation | convolution fusion | flops 3538944 | bytes 1310756 | tf_op jit(solution)/shard_map/dot_general | solution.py:134
  131.2 2.4 %fusion.2 = f32[1,8,32,128]{3,0,2,1:T(1,128)} fusion(f32[8,32,128,9]{2,1,0,3:T(8,128)S(1)} %bitcast.245, f32[9]{0:T(128)S(1)} %multiply_add_fusion, f32[9]{0:T(128)S(1)} %multiply_add_fusion.1, f32[9]{0:T(128)S(1)} %select_add_fusion, f32[]{:T(128)S(6)} %div.44, f32[]{:T(128)S(6)} %div.42, f32[]{:T(128)S(6)} %div.40, f32[]{:T(128)S(6)} %div.38), kind=kOutput, calls=%fused_computation.2 | convolution fusion | flops 3539016 | bytes 1310844 | tf_op jit(solution)/shard_map/dot_general | solution.py:133
  135.0 1.1 fusion.62
  (62 shorter events, 14.6 us)
Async XLA Ops:
  0.6 135.5 %copy-start = (f32[16,16]{1,0:T(8,128)S(1)}, f32[16,16]{1,0:T(8,128)}, u32[]{:S(2)}) copy-start(f32[16,16]{1,0:T(8,128)} %param.12) | copy-start | bytes 3076
  0.6 18.8 %copy-start.1 = (f32[8,32,128]{2,1,0:T(8,128)S(1)}, f32[8,32,128]{2,1,0:T(8,128)}, u32[]{:S(2)}) copy-start(f32[8,32,128]{2,1,0:T(8,128)} %param.8) | copy-start | bytes 393220
  0.7 18.8 %copy-start.2 = (f32[8,32,128]{2,1,0:T(8,128)S(1)}, f32[8,32,128]{2,1,0:T(8,128)}, u32[]{:S(2)}) copy-start(f32[8,32,128]{2,1,0:T(8,128)} %param.7) | copy-start | bytes 393220
  0.7 18.8 %copy-start.3 = (f32[8,32,128]{2,1,0:T(8,128)S(1)}, f32[8,32,128]{2,1,0:T(8,128)}, u32[]{:S(2)}) copy-start(f32[8,32,128]{2,1,0:T(8,128)} %param.9) | copy-start | bytes 393220
  1.8 5.8 %collective-permute-start = (f32[3,4,32,128]{3,2,1,0:T(8,128)S(1)}, f32[3,4,32,128]{3,2,1,0:T(8,128)S(1)}, u32[]{:S(2)}, u32[]{:S(2)}) collective-permute-start(f32[3,4,32,128]{3,2,1,0:T(8,128)S(1)} %get-tuple-element.13), channel_id=1, source_target_pairs={{0,8},{8,16},{16,24},{24,0},{1,9},{9,17},{17,25},{25,1},{2,10},{10... | collective-permute-start | bytes 589832 | tf_op jit(solution)/shard_map/ppermute | solution.py:19
  2.4 7.2 %collective-permute-start.1 = (f32[3,4,32,128]{3,2,1,0:T(8,128)S(1)}, f32[3,4,32,128]{3,2,1,0:T(8,128)S(1)}, u32[]{:S(2)}, u32[]{:S(2)}) collective-permute-start(f32[3,4,32,128]{3,2,1,0:T(8,128)S(1)} %get-tuple-element.14), channel_id=1, source_target_pairs={{8,0},{16,8},{24,16},{0,24},{9,1},{17,9},{25,17},{1,25},{10,2},{18... | collective-permute-start | bytes 589832 | tf_op jit(solution)/shard_map/ppermute | solution.py:22
  10.5 7.5 %collective-permute-start.2 = (f32[3,16,4,128]{3,2,1,0:T(4,128)S(1)}, f32[3,16,4,128]{3,2,1,0:T(4,128)S(1)}, u32[]{:S(2)}, u32[]{:S(2)}) collective-permute-start(f32[3,16,4,128]{3,2,1,0:T(4,128)S(1)} %get-tuple-element.11), channel_id=1, source_target_pairs={{0,2},{2,4},{4,6},{6,0},{1,3},{3,5},{5,7},{7,1},{8,10},{10,12},{12... | collective-permute-start | bytes 294920 | tf_op jit(solution)/shard_map/ppermute | solution.py:19
  12.1 7.3 %collective-permute-start.3 = (f32[3,16,4,128]{3,2,1,0:T(4,128)S(1)}, f32[3,16,4,128]{3,2,1,0:T(4,128)S(1)}, u32[]{:S(2)}, u32[]{:S(2)}) collective-permute-start(f32[3,16,4,128]{3,2,1,0:T(4,128)S(1)} %get-tuple-element.12), channel_id=1, source_target_pairs={{2,0},{4,2},{6,4},{0,6},{3,1},{5,3},{7,5},{1,7},{10,8},{12,10},{14... | collective-permute-start | bytes 294920 | tf_op jit(solution)/shard_map/ppermute | solution.py:22
  19.9 2.9 %copy-start.5 = (f32[9,9]{1,0:T(8,128)S(1)}, f32[9,9]{1,0:T(8,128)}, u32[]{:S(2)}) copy-start(f32[9,9]{1,0:T(8,128)} %constant.17.clone) | copy-start | bytes 976
  20.3 5.4 %collective-permute-start.4 = (f32[3,16,40,4]{2,1,3,0:T(8,128)S(1)}, f32[3,16,40,4]{2,1,3,0:T(8,128)S(1)}, u32[]{:S(2)}, u32[]{:S(2)}) collective-permute-start(f32[3,16,40,4]{2,1,3,0:T(8,128)S(1)} %copy.18), channel_id=1, source_target_pairs={{0,1},{1,0},{2,3},{3,2},{4,5},{5,4},{6,7},{7,6},{8,9},{9,8},{10,11... | collective-permute-start | bytes 92168 | tf_op jit(solution)/shard_map/ppermute | solution.py:19
  22.2 4.9 %collective-permute-start.5 = (f32[3,16,40,4]{2,1,3,0:T(8,128)S(1)}, f32[3,16,40,4]{2,1,3,0:T(8,128)S(1)}, u32[]{:S(2)}, u32[]{:S(2)}) collective-permute-start(f32[3,16,40,4]{2,1,3,0:T(8,128)S(1)} %copy.19), channel_id=1, source_target_pairs={{1,0},{0,1},{3,2},{2,3},{5,4},{4,5},{7,6},{6,7},{9,8},{8,9},{11,10... | collective-permute-start | bytes 92168 | tf_op jit(solution)/shard_map/ppermute | solution.py:22
  131.2 5.1 %copy-start.4 = (bf16[16,8,32,128]{3,2,1,0:T(8,128)(2,1)S(1)}, bf16[16,8,32,128]{3,2,1,0:T(8,128)(2,1)}, u32[]{:S(2)}) copy-start(bf16[16,8,32,128]{3,2,1,0:T(8,128)(2,1)} %param.10) | copy-start | bytes 3145732
